TPU v7x, 32 devices: a whole 2x2x4 slice. The times are simulated.
32 devices in a mesh: tm: 4 (over y, x), space: 8 (over z, core).
Axes of the slice: x: 2, y: 2, z: 4, core: 2. Of those that a mesh axis runs over, the one named last changes fastest.
Arguments:
- queries: bfloat16 [4096, 4096], P(('tm', 'space')), may hold values from -20 to 20
- key_vectors: bfloat16 [4096, 4096], P(('tm', 'space')), may hold values from -20 to 20
- value_vectors: bfloat16 [4096, 4096], P(('tm', 'space')), may hold values from -6 to 6
- out_weight: bfloat16 [4096, 6144], P(None, 'space'), may hold values from -0.375 to 0.375
- frame_mask: int32 [4, 4], replicated, may hold values 0 or 1
Outputs:
- projected: bfloat16 [4096, 6144], P('tm', 'space')
All inputs are finite; a program needn't handle non-finite values.
Results may differ from a plain program's by a relative error of at most 0.0075.
Values may be sent and summed in bfloat16 or wider, within the bound.
A program may use at most 128 MiB of HBM per device.

v0:
```python
import math
import jax
import jax.numpy as jnp
from jax import lax
from jax.sharding import PartitionSpec as P

HD = 128


def passed_along(x, axis, by):
    devices = lax.axis_size(axis)
    return lax.ppermute(x, axis, [(i, (i + by) % devices) for i in range(devices)])


def block_update(state, query_blocks, arrived, allowed, scale_factor):
    run_max, run_total, run_sum = state
    keys_here = arrived[0]
    values_here = arrived[1]

    def one_block(pieces):
        query_part, old_max, old_total, old_sum = pieces
        scores = (
            jnp.einsum("qhd,khd->qhk", query_part, keys_here, preferred_element_type=jnp.float32)
            * scale_factor
        )
        block_max = jnp.where(allowed, jnp.max(scores, axis=2), -jnp.inf)
        new_max = jnp.maximum(old_max, block_max)
        exp_terms = jnp.where(allowed, jnp.exp(scores - new_max[:, :, None]), 0.0)
        rescale = jnp.exp(old_max - new_max)
        new_total = old_total * rescale + jnp.sum(exp_terms, axis=2)
        new_sum = old_sum * rescale[:, :, None] + jnp.einsum(
            "qhk,khd->qhd",
            exp_terms.astype(jnp.bfloat16),
            values_here,
            preferred_element_type=jnp.float32,
        )
        return (new_max, new_total, new_sum)

    return lax.map(one_block, (query_blocks, run_max, run_total, run_sum))


def mask_bit(frame_mask, row_index, column_index):
    count = frame_mask.shape[0]
    grid_rows = lax.broadcasted_iota(jnp.int32, (count, count), 0)
    grid_cols = lax.broadcasted_iota(jnp.int32, (count, count), 1)
    return jnp.sum(jnp.where((grid_rows == row_index) & (grid_cols == column_index), frame_mask, 0))


def body(queries, key_vectors, value_vectors, out_weight, frame_mask):
    frames = lax.axis_size("tm")
    here = lax.axis_index("tm")
    head_queries, head_keys, head_values = (
        lax.all_to_all(queries, "space", split_axis=1, concat_axis=0, tiled=True),
        lax.all_to_all(key_vectors, "space", split_axis=1, concat_axis=0, tiled=True),
        lax.all_to_all(value_vectors, "space", split_axis=1, concat_axis=0, tiled=True),
    )
    row_count = head_queries.shape[0]
    local_heads = head_queries.shape[1] // HD
    scale_factor = 1.0 / math.sqrt(HD)
    block_rows = 512
    block_count = row_count // block_rows
    query_blocks = head_queries.reshape(block_count, block_rows, local_heads, HD)
    pair = jnp.stack([head_keys, head_values]).reshape(2, row_count, local_heads, HD)
    state = (
        jnp.full((block_count, block_rows, local_heads), -jnp.inf, jnp.float32),
        jnp.zeros((block_count, block_rows, local_heads), jnp.float32),
        jnp.zeros((block_count, block_rows, local_heads, HD), jnp.float32),
    )
    state = block_update(state, query_blocks, pair, True, scale_factor)

    def visit(current, arrived, source):
        source_block = jnp.mod(source, frames)
        granted = mask_bit(frame_mask, here, source_block) == 1
        return block_update(current, query_blocks, arrived, granted, scale_factor)

    lower = pair
    upper = pair
    lower = passed_along(lower, "tm", 1)
    upper = passed_along(upper, "tm", -1)
    state = visit(state, lower, here - 1)
    state = visit(state, upper, here + 1)
    run_max, run_total, run_sum = state
    attended = (
        (run_sum / run_total[:, :, :, None])
        .reshape(row_count, local_heads * HD)
        .astype(jnp.bfloat16)
    )
    projected = jnp.dot(
        lax.all_gather(attended, "space", axis=1, tiled=True),
        out_weight,
        preferred_element_type=jnp.float32,
    )
    return projected.astype(jnp.bfloat16)


def solution(mesh):
    in_specs = (
        P(("tm", "space"), None),
        P(("tm", "space"), None),
        P(("tm", "space"), None),
        P(None, "space"),
        P(),
    )
    out_specs = P("tm", "space")
    return jax.shard_map(body, mesh=mesh, in_specs=in_specs, out_specs=out_specs, check_vma=False)
```

profile of v0, /device:TPU:0, one launch (start us, length us, event | category | flops | bytes accessed | tf_op | source)
XLA Modules:
  0.0 311.0 jit_solution(401340638023929092)
XLA Ops:
  6.5 2.3 copy.20
  8.9 6.4 %all-to-all-start.1 = ((bf16[128,8,512]{0,2,1:T(8,128)(2,1)}), bf16[128,8,512]{0,2,1:T(8,128)(2,1)S(1)}, u32[]{:S(2)}, u32[]{:S(2)}) async-start(bf16[128,8,512]{0,2,1:T(8,128)(2,1)} %bitcast.23), calls=%async_computation.1 | async-start | bytes 2097152 | tf_op jit(solution)/shard_map/all_to_all | solution.py:54
  15.2 2.3 copy.22
  17.5 24.3 %all-to-all-done.1 = bf16[128,8,512]{0,2,1:T(8,128)(2,1)S(1)} async-done(((bf16[128,8,512]{0,2,1:T(8,128)(2,1)}), bf16[128,8,512]{0,2,1:T(8,128)(2,1)S(1)}, u32[]{:S(2)}, u32[]{:S(2)}) %all-to-all-start.1) | async-done | bytes 1048608 | tf_op jit(solution)/shard_map/all_to_all | solution.py:54
  41.8 3.6 %all-to-all-start.2 = ((bf16[128,8,512]{0,2,1:T(8,128)(2,1)}), bf16[128,8,512]{0,2,1:T(8,128)(2,1)S(1)}, u32[]{:S(2)}, u32[]{:S(2)}) async-start(bf16[128,8,512]{0,2,1:T(8,128)(2,1)} %bitcast.25), calls=%async_computation.2 | async-start | bytes 2097152 | tf_op jit(solution)/shard_map/all_to_all | solution.py:55
  46.4 25.4 %all-to-all-done.2 = bf16[128,8,512]{0,2,1:T(8,128)(2,1)S(1)} async-done(((bf16[128,8,512]{0,2,1:T(8,128)(2,1)}), bf16[128,8,512]{0,2,1:T(8,128)(2,1)S(1)}, u32[]{:S(2)}, u32[]{:S(2)}) %all-to-all-start.2) | async-done | bytes 1048608 | tf_op jit(solution)/shard_map/all_to_all | solution.py:55
  72.8 3.6 %all-to-all-start = ((bf16[128,8,512]{2,0,1:T(8,128)(2,1)}), bf16[128,8,512]{2,0,1:T(8,128)(2,1)S(1)}, u32[]{:S(2)}, u32[]{:S(2)}) async-start(bf16[128,8,512]{2,0,1:T(8,128)(2,1)} %bitcast.193), calls=%async_computation | async-start | bytes 2097152 | tf_op jit(solution)/shard_map/all_to_all | solution.py:53
  81.8 2.0 copy.23
  86.3 2.3 constant_dynamic-update-slice_fusion.1
  88.6 2.3 constant_dynamic-update-slice_fusion
  90.9 1.5 collective-permute-start
  92.4 1.4 collective-permute-start.1
  93.8 9.1 %all-to-all-done = bf16[128,8,512]{2,0,1:T(8,128)(2,1)S(1)} async-done(((bf16[128,8,512]{2,0,1:T(8,128)(2,1)}), bf16[128,8,512]{2,0,1:T(8,128)(2,1)S(1)}, u32[]{:S(2)}, u32[]{:S(2)}) %all-to-all-start) | async-done | bytes 1048608 | tf_op jit(solution)/shard_map/all_to_all | solution.py:53
  104.0 1.6 copy.26
  105.6 1.5 broadcast.129.clone.1
  107.1 11.4 %while.40 = (s32[]{:T(128)}, f32[2,512,4]{1,2,0:T(4,128)S(1)}, f32[2,512,4]{1,2,0:T(4,128)S(1)}, f32[2,512,4,128]{3,1,2,0:T(8,128)}, bf16[2,512,4,128]{3,1,2,0:T...) while((s32[]{:T(128)}, f32[2,512,4]{1,2,0:T(4,128)S(1)}, ...), condition=%wide.region_3.4_spmd, body=%wide.region_0.3_spmd.sunk | while | flops 1090787328 | bytes 45703320 | solution.py:39
  107.1 1.3 bitcast_reduce_fusion.6
  108.7 2.2 fusion.118
  110.9 1.9 fusion.116
  112.9 1.3 bitcast_reduce_fusion.6
  114.5 2.2 fusion.118
  116.7 1.9 fusion.116
  118.6 22.0 %collective-permute-done = bf16[2,1024,4,128]{1,3,2,0:T(8,128)(2,1)} collective-permute-done((bf16[2,1024,4,128]{1,3,2,0:T(8,128)(2,1)}, bf16[2,1024,4,128]{1,3,2,0:T(8,128)(2,1)}, u32[]{:S(2)}, u32[]{:S(2)}) %collective-permute-start) | collective-permute-done | bytes 2097184 | tf_op jit(solution)/shard_map/ppermute | solution.py:12
  140.6 2.8 slice_bitcast_fusion.2
  143.4 1.6 copy.30
  145.0 1.3 copy.31
  146.3 1.5 broadcast.129.clone
  147.8 13.7 %while.41 = (s32[]{:T(128)}, f32[2,512,4]{1,2,0:T(4,128)S(1)}, f32[2,512,4]{1,2,0:T(4,128)S(1)}, f32[2,512,4,128]{3,1,2,0:T(8,128)}, f32[2,512,4]{1,2,0:T(4,128)...) while((s32[]{:T(128)}, f32[2,512,4]{1,2,0:T(4,128)S(1)}, ...), condition=%wide.region_8.9_spmd, body=%wide.region_5.8_spmd.sunk | while | flops 1095249920 | bytes 59367672 | solution.py:39
  147.8 1.3 bitcast_reduce_fusion.7
  150.3 2.2 fusion.125
  152.5 2.1 fusion.123
  154.7 1.3 bitcast_reduce_fusion.7
  157.2 2.2 fusion.125
  159.4 2.1 fusion.123
  161.5 23.4 %collective-permute-done.1 = bf16[2,1024,4,128]{1,3,2,0:T(8,128)(2,1)} collective-permute-done((bf16[2,1024,4,128]{1,3,2,0:T(8,128)(2,1)}, bf16[2,1024,4,128]{1,3,2,0:T(8,128)(2,1)}, u32[]{:S(2)}, u32[]{:S(2)}) %collective-permute-start.1) | collective-permute-done | bytes 2097184 | tf_op jit(solution)/shard_map/ppermute | solution.py:12
  185.0 2.8 slice_bitcast_fusion
  187.7 1.6 copy.33
  190.7 1.5 broadcast.129
  192.2 13.7 %while.42 = (s32[]{:T(128)}, f32[2,512,4]{1,2,0:T(4,128)S(1)}, f32[2,512,4,128]{3,1,2,0:T(8,128)}, f32[2,512,4]{1,2,0:T(4,128)S(1)}, f32[2,512,4]{1,2,0:T(4,128)...) while((s32[]{:T(128)}, f32[2,512,4]{1,2,0:T(4,128)S(1)}, ...), condition=%wide.region_13.14_spmd, body=%wide.region_10.13_spmd.sunk | while | flops 1095249920 | bytes 59359472 | solution.py:39
  192.2 1.3 bitcast_reduce_fusion.8
  194.7 2.2 fusion.132
  196.9 2.1 fusion.130
  199.1 1.3 bitcast_reduce_fusion.8
  201.5 2.2 fusion.132
  203.8 2.1 fusion.130
  205.9 2.2 divide_convert_fusion
  210.1 82.4 %all-gather.2.cloned.1.call-done = bf16[1024,4096]{1,0:T(8,128)(2,1)} async-done(((bf16[1024,512]{1,0:T(8,128)(2,1)}), bf16[1024,4096]{1,0:T(8,128)(2,1)}) %all-gather.2.cloned.1.call-update) | async-done | bytes 8388624 | tf_op jit(solution)/shard_map/all_gather | solution.py:89
  292.4 11.8 %convolution_convert_fusion = bf16[1024,768]{1,0:T(8,128)(2,1)} fusion(bf16[1024,4096]{1,0:T(8,128)(2,1)} %all-gather.2.cloned.1.call-done, bf16[4096,768]{1,0:T(8,128)(2,1)} %param.14), kind=kOutput, calls=%fused_computation.78 | convolution fusion | flops 6443237376 | bytes 16252928 | tf_op jit(solution)/shard_map/dot_general | solution.py:88
  (82 shorter events, 18.1 us)
Async XLA Ops:
  6.5 38.8 %copy-start.10 = (bf16[128,4096]{1,0:T(8,128)(2,1)S(1)}, bf16[128,4096]{1,0:T(8,128)(2,1)}, u32[]{:S(2)}) copy-start(bf16[128,4096]{1,0:T(8,128)(2,1)} %param.11) | copy-start | bytes 3145732
  6.5 70.0 %copy-start.13 = (s32[4,4]{1,0:T(4,128)S(1)}, s32[4,4]{1,0:T(4,128)}, u32[]{:S(2)}) copy-start(s32[4,4]{1,0:T(4,128)} %param.15) | copy-start | bytes 196
  8.9 32.9 %all-to-all-start.1 = ((bf16[128,8,512]{0,2,1:T(8,128)(2,1)}), bf16[128,8,512]{0,2,1:T(8,128)(2,1)S(1)}, u32[]{:S(2)}, u32[]{:S(2)}) async-start(bf16[128,8,512]{0,2,1:T(8,128)(2,1)} %bitcast.23), calls=%async_computation.1 | async-start | bytes 2097152 | tf_op jit(solution)/shard_map/all_to_all | solution.py:54
  41.8 30.1 %all-to-all-start.2 = ((bf16[128,8,512]{0,2,1:T(8,128)(2,1)}), bf16[128,8,512]{0,2,1:T(8,128)(2,1)S(1)}, u32[]{:S(2)}, u32[]{:S(2)}) async-start(bf16[128,8,512]{0,2,1:T(8,128)(2,1)} %bitcast.25), calls=%async_computation.2 | async-start | bytes 2097152 | tf_op jit(solution)/shard_map/all_to_all | solution.py:55
  71.9 1.0 copy-start.2
  72.8 30.1 %all-to-all-start = ((bf16[128,8,512]{2,0,1:T(8,128)(2,1)}), bf16[128,8,512]{2,0,1:T(8,128)(2,1)S(1)}, u32[]{:S(2)}, u32[]{:S(2)}) async-start(bf16[128,8,512]{2,0,1:T(8,128)(2,1)} %bitcast.193), calls=%async_computation | async-start | bytes 2097152 | tf_op jit(solution)/shard_map/all_to_all | solution.py:53
  76.4 216.0 %all-gather.2.cloned.1.call-start = ((), (), s32[]{:S(2)}) async-start(), calls=%async_computation.3 | async-start | bytes 9437184 | tf_op jit(solution)/shard_map/all_gather | solution.py:89
  81.8 21.6 %copy-start.3 = (bf16[1024,4,128]{0,2,1:T(8,128)(2,1)S(1)}, bf16[1024,4,128]{0,2,1:T(8,128)(2,1)}, u32[]{:S(2)}) copy-start(bf16[1024,4,128]{0,2,1:T(8,128)(2,1)} %squeeze.55) | copy-start | bytes 3145732
  90.9 49.7 %collective-permute-start = (bf16[2,1024,4,128]{1,3,2,0:T(8,128)(2,1)}, bf16[2,1024,4,128]{1,3,2,0:T(8,128)(2,1)}, u32[]{:S(2)}, u32[]{:S(2)}) collective-permute-start(bf16[2,1024,4,128]{1,3,2,0:T(8,128)(2,1)} %constant_dynamic-update-slice_fusion), channel_id=1, source_target_pairs={{0,8},{8,16},{16,24},{24,0},{1,9},{9,17},{17,25},{25,1},{2,10},{10... | collective-permute-start | bytes 6291464 | tf_op jit(solution)/shard_map/ppermute | solution.py:12
  92.4 92.6 %collective-permute-start.1 = (bf16[2,1024,4,128]{1,3,2,0:T(8,128)(2,1)}, bf16[2,1024,4,128]{1,3,2,0:T(8,128)(2,1)}, u32[]{:S(2)}, u32[]{:S(2)}) collective-permute-start(bf16[2,1024,4,128]{1,3,2,0:T(8,128)(2,1)} %constant_dynamic-update-slice_fusion), channel_id=1, source_target_pairs={{0,24},{8,0},{16,8},{24,16},{1,25},{9,1},{17,9},{25,17},{2,26},{10... | collective-permute-start | bytes 6291464 | tf_op jit(solution)/shard_map/ppermute | solution.py:12
  107.1 1.6 copy-start.4
  110.9 1.9 copy-start.5
  112.9 1.6 copy-start.4
  116.7 1.9 copy-start.5
  147.8 1.6 copy-start.6
  147.8 2.2 copy-start.7
  147.8 2.5 copy-start.11
  152.5 2.1 copy-start.8
  154.7 1.6 copy-start.6
  154.7 2.2 copy-start.7
  154.7 2.5 copy-start.11
  159.4 2.1 copy-start.8
  192.2 1.6 copy-start
  192.2 2.2 copy-start.9
  192.2 2.5 copy-start.12
  196.9 2.1 copy-start.1
  199.0 1.6 copy-start
  199.0 2.2 copy-start.9
  199.1 2.5 copy-start.12
  203.8 2.1 copy-start.1
Sparse Core Ops, SparseCore 0:
  210.2 82.1 all-gather.1
where the time goes:
time: 312 us; the launch traced here: 311 us
  waiting for transfers between devices  187 us (60%)
  local copies, waits for them, and re-layouts  44.5 us (14%)
  matrix products  33.1 us (11%)
  starting transfers between devices  16.4 us (5%)
  other arithmetic  15.2 us (5%)
  between operations  14.9 us (5%)
    all_gather x1, waiting for transfers between devices, body(): lax.all_gather(attended, 'space', axis=1, tiled=True)  82.4 us
    ppermute x2, waiting for transfers between devices, passed_along(): lax.ppermute(x, axis, [(i, (i + by) % devices) for i in range(devices)])  45.5 us
    all_to_all x1, waiting for transfers between devices, body(): lax.all_to_all(value_vectors, 'space', split_axis=1, concat_axis=0, tiled...  25.4 us
    all_to_all x1, waiting for transfers between devices, body(): lax.all_to_all(key_vectors, 'space', split_axis=1, concat_axis=0, tiled=T...  24.3 us
    dot_general x6, matrix products, one_block(): jnp.einsum('qhk,khd->qhd', exp_terms.astype(jnp.bfloat16), values_here, p...  13.3 us
    reduce_sum x6, other arithmetic, one_block(): new_total = old_total * rescale + jnp.sum(exp_terms, axis=2)  12 us
    dot_general x1, matrix products, body(): jnp.dot(lax.all_gather(attended, 'space', axis=1, tiled=True), out_weight...  11.8 us
    all_to_all x1, waiting for transfers between devices, body(): lax.all_to_all(queries, 'space', split_axis=1, concat_axis=0, tiled=True)  9.06 us
  transfers between devices with their start and end apart: 6, of which 6 were waited for; matrix products, arithmetic and copies ran while one was open for 16% of the time, Pallas kernels for 0%

commit v1 on v0

--- a/solution.py
+++ b/solution.py
@@ -5,6 +5,11 @@
 from jax.sharding import PartitionSpec as P
 
 HD = 128
+
+
+def stack_and_merge(x, mesh_axis, dim):
+    pieces = lax.all_gather(x, mesh_axis)
+    return jnp.concatenate(pieces, axis=dim)
 
 
 def passed_along(x, axis, by):
@@ -86,9 +91,7 @@
         .astype(jnp.bfloat16)
     )
     projected = jnp.dot(
-        lax.all_gather(attended, "space", axis=1, tiled=True),
-        out_weight,
-        preferred_element_type=jnp.float32,
+        stack_and_merge(attended, "space", 1), out_weight, preferred_element_type=jnp.float32
     )
     return projected.astype(jnp.bfloat16)
 

time: 312 us -> 324 us (1.038)
  local copies, waits for them, and re-layouts: 44.5 us -> 56 us
    all_gather x0 -> x1, local copies, waits for them, and re-layouts: none -> 11.4 us  [stack_and_merge(): pieces = lax.all_gather(x, mesh_axis)]
    unnamed x12 -> x11, local copies, waits for them, and re-layouts: 9.05 us -> 7.9 us
where the time goes in v1:
time: 324 us; the launch traced here: 323 us
  waiting for transfers between devices  187 us (58%)
  local copies, waits for them, and re-layouts  56 us (17%)
  matrix products  33.2 us (10%)
  starting transfers between devices  16.4 us (5%)
  other arithmetic  15.2 us (5%)
  between operations  14.9 us (5%)
    all_gather x1, waiting for transfers between devices, stack_and_merge(): pieces = lax.all_gather(x, mesh_axis)  82.4 us
    ppermute x2, waiting for transfers between devices, passed_along(): lax.ppermute(x, axis, [(i, (i + by) % devices) for i in range(devices)])  45.5 us
    all_to_all x1, waiting for transfers between devices, body(): lax.all_to_all(value_vectors, 'space', split_axis=1, concat_axis=0, tiled...  25.4 us
    all_to_all x1, waiting for transfers between devices, body(): lax.all_to_all(key_vectors, 'space', split_axis=1, concat_axis=0, tiled=T...  24.3 us
    dot_general x6, matrix products, one_block(): jnp.einsum('qhk,khd->qhd', exp_terms.astype(jnp.bfloat16), values_here, p...  13.3 us
    reduce_sum x6, other arithmetic, one_block(): new_total = old_total * rescale + jnp.sum(exp_terms, axis=2)  12 us
    dot_general x1, matrix products, body(): jnp.dot(stack_and_merge(attended, 'space', 1), out_weight, preferred_elem...  11.9 us
    all_gather x1, local copies, waits for them, and re-layouts, stack_and_merge(): pieces = lax.all_gather(x, mesh_axis)  11.4 us
  transfers between devices with their start and end apart: 6, of which 6 were waited for; matrix products, arithmetic and copies ran while one was open for 16% of the time, Pallas kernels for 0%

profile of v1, /device:TPU:0, one launch (start us, length us, event | category | flops | bytes accessed | tf_op | source)
XLA Modules:
  0.0 322.7 jit_solution(17438830157324887424)
XLA Ops:
  6.5 2.3 copy.21
  8.9 6.4 %all-to-all-start.1 = ((bf16[128,8,512]{0,2,1:T(8,128)(2,1)}), bf16[128,8,512]{0,2,1:T(8,128)(2,1)S(1)}, u32[]{:S(2)}, u32[]{:S(2)}) async-start(bf16[128,8,512]{0,2,1:T(8,128)(2,1)} %bitcast.23), calls=%async_computation.1 | async-start | bytes 2097152 | tf_op jit(solution)/shard_map/all_to_all | solution.py:59
  15.2 2.3 copy.23
  17.5 24.3 %all-to-all-done.1 = bf16[128,8,512]{0,2,1:T(8,128)(2,1)S(1)} async-done(((bf16[128,8,512]{0,2,1:T(8,128)(2,1)}), bf16[128,8,512]{0,2,1:T(8,128)(2,1)S(1)}, u32[]{:S(2)}, u32[]{:S(2)}) %all-to-all-start.1) | async-done | bytes 1048608 | tf_op jit(solution)/shard_map/all_to_all | solution.py:59
  41.8 3.6 %all-to-all-start.2 = ((bf16[128,8,512]{0,2,1:T(8,128)(2,1)}), bf16[128,8,512]{0,2,1:T(8,128)(2,1)S(1)}, u32[]{:S(2)}, u32[]{:S(2)}) async-start(bf16[128,8,512]{0,2,1:T(8,128)(2,1)} %bitcast.25), calls=%async_computation.2 | async-start | bytes 2097152 | tf_op jit(solution)/shard_map/all_to_all | solution.py:60
  46.4 25.4 %all-to-all-done.2 = bf16[128,8,512]{0,2,1:T(8,128)(2,1)S(1)} async-done(((bf16[128,8,512]{0,2,1:T(8,128)(2,1)}), bf16[128,8,512]{0,2,1:T(8,128)(2,1)S(1)}, u32[]{:S(2)}, u32[]{:S(2)}) %all-to-all-start.2) | async-done | bytes 1048608 | tf_op jit(solution)/shard_map/all_to_all | solution.py:60
  72.8 3.6 %all-to-all-start = ((bf16[128,8,512]{2,0,1:T(8,128)(2,1)}), bf16[128,8,512]{2,0,1:T(8,128)(2,1)S(1)}, u32[]{:S(2)}, u32[]{:S(2)}) async-start(bf16[128,8,512]{2,0,1:T(8,128)(2,1)} %bitcast.191), calls=%async_computation | async-start | bytes 2097152 | tf_op jit(solution)/shard_map/all_to_all | solution.py:58
  81.8 2.0 copy.24
  86.3 2.3 constant_dynamic-update-slice_fusion.1
  88.6 2.3 constant_dynamic-update-slice_fusion
  90.9 1.5 collective-permute-start
  92.4 1.4 collective-permute-start.1
  93.8 9.1 %all-to-all-done = bf16[128,8,512]{2,0,1:T(8,128)(2,1)S(1)} async-done(((bf16[128,8,512]{2,0,1:T(8,128)(2,1)}), bf16[128,8,512]{2,0,1:T(8,128)(2,1)S(1)}, u32[]{:S(2)}, u32[]{:S(2)}) %all-to-all-start) | async-done | bytes 1048608 | tf_op jit(solution)/shard_map/all_to_all | solution.py:58
  104.0 1.6 copy.27
  105.6 1.5 broadcast.129.clone.1
  107.1 11.4 %while.40 = (s32[]{:T(128)}, f32[2,512,4]{1,2,0:T(4,128)S(1)}, f32[2,512,4]{1,2,0:T(4,128)S(1)}, f32[2,512,4,128]{3,1,2,0:T(8,128)}, bf16[2,512,4,128]{3,1,2,0:T...) while((s32[]{:T(128)}, f32[2,512,4]{1,2,0:T(4,128)S(1)}, ...), condition=%wide.region_3.4_spmd, body=%wide.region_0.3_spmd.sunk | while | flops 1090787328 | bytes 45703320 | solution.py:44
  107.1 1.3 bitcast_reduce_fusion.6
  108.7 2.2 fusion.118
  110.9 1.9 fusion.116
  112.9 1.3 bitcast_reduce_fusion.6
  114.5 2.2 fusion.118
  116.7 1.9 fusion.116
  118.6 22.0 %collective-permute-done = bf16[2,1024,4,128]{1,3,2,0:T(8,128)(2,1)} collective-permute-done((bf16[2,1024,4,128]{1,3,2,0:T(8,128)(2,1)}, bf16[2,1024,4,128]{1,3,2,0:T(8,128)(2,1)}, u32[]{:S(2)}, u32[]{:S(2)}) %collective-permute-start) | collective-permute-done | bytes 2097184 | tf_op jit(solution)/shard_map/ppermute | solution.py:17
  140.6 2.8 slice_bitcast_fusion.2
  143.4 1.6 copy.31
  146.3 1.5 broadcast.129.clone
  147.8 13.7 %while.41 = (s32[]{:T(128)}, f32[2,512,4]{1,2,0:T(4,128)S(1)}, f32[2,512,4]{1,2,0:T(4,128)S(1)}, f32[2,512,4,128]{3,1,2,0:T(8,128)}, f32[2,512,4]{1,2,0:T(4,128)...) while((s32[]{:T(128)}, f32[2,512,4]{1,2,0:T(4,128)S(1)}, ...), condition=%wide.region_8.9_spmd, body=%wide.region_5.8_spmd.sunk | while | flops 1095249920 | bytes 59367672 | solution.py:44
  147.8 1.3 bitcast_reduce_fusion.7
  150.3 2.2 fusion.125
  152.5 2.1 fusion.123
  154.7 1.3 bitcast_reduce_fusion.7
  157.2 2.2 fusion.125
  159.4 2.1 fusion.123
  161.5 23.4 %collective-permute-done.1 = bf16[2,1024,4,128]{1,3,2,0:T(8,128)(2,1)} collective-permute-done((bf16[2,1024,4,128]{1,3,2,0:T(8,128)(2,1)}, bf16[2,1024,4,128]{1,3,2,0:T(8,128)(2,1)}, u32[]{:S(2)}, u32[]{:S(2)}) %collective-permute-start.1) | collective-permute-done | bytes 2097184 | tf_op jit(solution)/shard_map/ppermute | solution.py:17
  185.0 2.8 slice_bitcast_fusion
  187.7 1.6 copy.34
  190.7 1.5 broadcast.129
  192.2 13.7 %while.42 = (s32[]{:T(128)}, f32[2,512,4]{1,2,0:T(4,128)S(1)}, f32[2,512,4,128]{3,1,2,0:T(8,128)}, f32[2,512,4]{1,2,0:T(4,128)S(1)}, f32[2,512,4]{1,2,0:T(4,128)...) while((s32[]{:T(128)}, f32[2,512,4]{1,2,0:T(4,128)S(1)}, ...), condition=%wide.region_13.14_spmd, body=%wide.region_10.13_spmd.sunk | while | flops 1095249920 | bytes 59359472 | solution.py:44
  192.2 1.3 bitcast_reduce_fusion.8
  194.7 2.2 fusion.132
  196.9 2.1 fusion.130
  199.1 1.3 bitcast_reduce_fusion.8
  201.5 2.2 fusion.132
  203.8 2.1 fusion.130
  205.9 2.2 divide_convert_fusion
  210.1 82.4 %all-gather.2.cloned.1.call-done = bf16[8,1024,512]{2,1,0:T(8,128)(2,1)} async-done(((bf16[1,1024,512]{2,1,0:T(8,128)(2,1)}), bf16[8,1024,512]{2,1,0:T(8,128)(2,1)}) %all-gather.2.cloned.1.call-update) | async-done | bytes 8388624 | tf_op jit(solution)/shard_map/all_gather | solution.py:11
  292.5 11.4 %copy.37 = bf16[8,1024,512]{1,2,0:T(8,128)(2,1)} copy(bf16[8,1024,512]{2,1,0:T(8,128)(2,1)} %all-gather.2.cloned.1.call-done) | data formatting | bytes 16777216 | tf_op jit(solution)/shard_map/all_gather | solution.py:11
  303.9 11.9 %convolution_convert_fusion = bf16[1024,768]{1,0:T(8,128)(2,1)} fusion(bf16[1024,4096]{0,1:T(8,128)(2,1)} %bitcast.260, bf16[4096,768]{1,0:T(8,128)(2,1)} %param.14), kind=kOutput, calls=%fused_computation.78 | convolution fusion | flops 6443237376 | bytes 16252928 | tf_op jit(solution)/shard_map/dot_general | solution.py:93
  (83 shorter events, 19.5 us)
Async XLA Ops:
  6.5 38.8 %copy-start.10 = (bf16[128,4096]{1,0:T(8,128)(2,1)S(1)}, bf16[128,4096]{1,0:T(8,128)(2,1)}, u32[]{:S(2)}) copy-start(bf16[128,4096]{1,0:T(8,128)(2,1)} %param.11) | copy-start | bytes 3145732
  6.5 70.0 %copy-start.13 = (s32[4,4]{1,0:T(4,128)S(1)}, s32[4,4]{1,0:T(4,128)}, u32[]{:S(2)}) copy-start(s32[4,4]{1,0:T(4,128)} %param.15) | copy-start | bytes 196
  8.9 32.9 %all-to-all-start.1 = ((bf16[128,8,512]{0,2,1:T(8,128)(2,1)}), bf16[128,8,512]{0,2,1:T(8,128)(2,1)S(1)}, u32[]{:S(2)}, u32[]{:S(2)}) async-start(bf16[128,8,512]{0,2,1:T(8,128)(2,1)} %bitcast.23), calls=%async_computation.1 | async-start | bytes 2097152 | tf_op jit(solution)/shard_map/all_to_all | solution.py:59
  41.8 30.1 %all-to-all-start.2 = ((bf16[128,8,512]{0,2,1:T(8,128)(2,1)}), bf16[128,8,512]{0,2,1:T(8,128)(2,1)S(1)}, u32[]{:S(2)}, u32[]{:S(2)}) async-start(bf16[128,8,512]{0,2,1:T(8,128)(2,1)} %bitcast.25), calls=%async_computation.2 | async-start | bytes 2097152 | tf_op jit(solution)/shard_map/all_to_all | solution.py:60
  71.9 1.0 copy-start.2
  72.8 30.1 %all-to-all-start = ((bf16[128,8,512]{2,0,1:T(8,128)(2,1)}), bf16[128,8,512]{2,0,1:T(8,128)(2,1)S(1)}, u32[]{:S(2)}, u32[]{:S(2)}) async-start(bf16[128,8,512]{2,0,1:T(8,128)(2,1)} %bitcast.191), calls=%async_computation | async-start | bytes 2097152 | tf_op jit(solution)/shard_map/all_to_all | solution.py:58
  76.4 216.1 %all-gather.2.cloned.1.call-start = ((), (), s32[]{:S(2)}) async-start(), calls=%async_computation.3 | async-start | bytes 9437184 | tf_op jit(solution)/shard_map/all_gather | solution.py:11
  81.8 21.6 %copy-start.3 = (bf16[1024,4,128]{0,2,1:T(8,128)(2,1)S(1)}, bf16[1024,4,128]{0,2,1:T(8,128)(2,1)}, u32[]{:S(2)}) copy-start(bf16[1024,4,128]{0,2,1:T(8,128)(2,1)} %squeeze.55) | copy-start | bytes 3145732
  90.9 49.7 %collective-permute-start = (bf16[2,1024,4,128]{1,3,2,0:T(8,128)(2,1)}, bf16[2,1024,4,128]{1,3,2,0:T(8,128)(2,1)}, u32[]{:S(2)}, u32[]{:S(2)}) collective-permute-start(bf16[2,1024,4,128]{1,3,2,0:T(8,128)(2,1)} %constant_dynamic-update-slice_fusion), channel_id=1, source_target_pairs={{0,8},{8,16},{16,24},{24,0},{1,9},{9,17},{17,25},{25,1},{2,10},{10... | collective-permute-start | bytes 6291464 | tf_op jit(solution)/shard_map/ppermute | solution.py:17
  92.4 92.6 %collective-permute-start.1 = (bf16[2,1024,4,128]{1,3,2,0:T(8,128)(2,1)}, bf16[2,1024,4,128]{1,3,2,0:T(8,128)(2,1)}, u32[]{:S(2)}, u32[]{:S(2)}) collective-permute-start(bf16[2,1024,4,128]{1,3,2,0:T(8,128)(2,1)} %constant_dynamic-update-slice_fusion), channel_id=1, source_target_pairs={{0,24},{8,0},{16,8},{24,16},{1,25},{9,1},{17,9},{25,17},{2,26},{10... | collective-permute-start | bytes 6291464 | tf_op jit(solution)/shard_map/ppermute | solution.py:17
  107.1 1.6 copy-start.4
  110.9 1.9 copy-start.5
  112.9 1.6 copy-start.4
  116.7 1.9 copy-start.5
  147.8 1.6 copy-start.6
  147.8 2.2 copy-start.7
  147.8 2.5 copy-start.11
  152.5 2.1 copy-start.8
  154.7 1.6 copy-start.6
  154.7 2.2 copy-start.7
  154.7 2.5 copy-start.11
  159.4 2.1 copy-start.8
  192.2 1.6 copy-start
  192.2 2.2 copy-start.9
  192.2 2.5 copy-start.12
  196.9 2.1 copy-start.1
  199.0 1.6 copy-start
  199.0 2.2 copy-start.9
  199.1 2.5 copy-start.12
  203.8 2.1 copy-start.1
Sparse Core Ops, SparseCore 0:
  210.3 82.1 all-gather.1
